TPU v7x, 32 devices: a whole 2x2x4 slice. The times are simulated.
32 devices in a mesh: dp: 4 (over y, x), seq: 4 (over z), grp: 2 (over core).
Axes of the slice: x: 2, y: 2, z: 4, core: 2. Of those that a mesh axis runs over, the one named last changes fastest.
Arguments:
- text_proj: bfloat16 [3, 16, 12, 128, 128], P(None, 'dp', None, ('seq', 'grp')), may hold values from -50 to 50
- image_proj: bfloat16 [3, 16, 12, 160, 128], P(None, ('dp', 'seq'), None, 'grp'), may hold values from -50 to 50
- text_grad: bfloat16 [16, 12, 128, 128], P('dp', None, ('seq', 'grp')), may hold values from -15 to 15
- image_grad: bfloat16 [16, 12, 160, 128], P(('dp', 'seq'), None, 'grp'), may hold values from -15 to 15
- text_lengths: int32 [16], P(('dp', 'seq')), may hold values from 1 to 128
- norm_gains: float32 [2, 2, 128], replicated, may hold values from 0.7 to 5.2
Outputs:
- text_out: bfloat16 [16, 12, 128, 128], P('dp', None, ('seq', 'grp'))
- image_out: bfloat16 [16, 12, 160, 128], P(('dp', 'seq'), None, 'grp')
- text_proj_grad: bfloat16 [3, 16, 12, 128, 128], P(None, 'dp', None, ('seq', 'grp'))
- image_proj_grad: bfloat16 [3, 16, 12, 160, 128], P(None, ('dp', 'seq'), None, 'grp')
- gain_grad: float32 [2, 2, 128], replicated
All inputs are finite; a program needn't handle non-finite values.
Results may differ from a plain program's by a relative error of at most 0.025.
The roundings to bfloat16 on the way count: a program that leaves them out, or rounds other values in their place, can miss the bound.
Values may be sent and summed in bfloat16 or wider, within the bound.
No kernel may reach another device: no remote copies, remote signals or barrier semaphores. Data moves between devices by JAX's collectives and lax.ppermute only.
A program may use at most 64 MiB of HBM per device.

v0:
```python
import jax
import jax.numpy as jnp
from jax import lax
from jax.sharding import PartitionSpec as P

TXT = 128
EPSILON = 1e-06
MASKED = -1e30


def forward(queries, key_rows, value_rows, key_valid):
    factor = queries.shape[-1] ** (-0.5)
    scores = (
        jnp.einsum("nqd,nkd->nqk", queries, key_rows, preferred_element_type=jnp.float32) * factor
    )
    scores = jnp.where(key_valid[:, None, :], scores, MASKED)
    row_max = jnp.max(scores, axis=-1, keepdims=True)
    exponent = jnp.exp(scores - row_max)
    attn_probs = exponent / jnp.sum(exponent, axis=-1, keepdims=True)
    rounded_probs = attn_probs.astype(jnp.bfloat16)
    attn_local = jnp.einsum(
        "nqk,nkd->nqd", rounded_probs, value_rows, preferred_element_type=jnp.float32
    )
    return (attn_probs, rounded_probs, attn_local)


def backward_terms(queries, key_rows, value_rows, attn_probs, rounded_probs, grad_out):
    factor = queries.shape[-1] ** (-0.5)
    grad_value = jnp.einsum(
        "nqk,nqd->nkd", rounded_probs, grad_out, preferred_element_type=jnp.float32
    )
    grad_probs = jnp.einsum(
        "nqd,nkd->nqk", grad_out, value_rows, preferred_element_type=jnp.float32
    )
    row_delta = jnp.sum(attn_probs * grad_probs, axis=-1, keepdims=True)
    grad_scores = (attn_probs * (grad_probs - row_delta) * factor).astype(jnp.bfloat16)
    grad_query = jnp.einsum(
        "nqk,nkd->nqd", grad_scores, key_rows, preferred_element_type=jnp.float32
    ).astype(jnp.bfloat16)
    grad_key = jnp.einsum("nqk,nqd->nkd", grad_scores, queries, preferred_element_type=jnp.float32)
    return (grad_query, grad_key, grad_value)


def sums_item(packed):
    query_one, key_one, value_one, valid_one, grad_one = packed
    attn_probs, rounded_probs, attn_local = forward(
        query_one[None], key_one[None], value_one[None], valid_one[None]
    )
    grad_query, grad_key, grad_value = backward_terms(
        query_one[None], key_one[None], value_one[None], attn_probs, rounded_probs, grad_one[None]
    )
    return (attn_local[0].astype(jnp.bfloat16), grad_query[0], grad_key[0], grad_value[0])


def whole_item(packed):
    attn_local, grad_query, grad_key, grad_value = sums_item(packed)
    return (attn_local, grad_query, grad_key.astype(jnp.bfloat16), grad_value.astype(jnp.bfloat16))


def unit_parts(raw_bf):
    raw_vals = raw_bf.astype(jnp.float32)
    inverse = lax.rsqrt(jnp.mean(raw_vals * raw_vals, axis=-1, keepdims=True) + EPSILON)
    return (raw_vals * inverse, inverse)


def raw_gradient(grad_normed_bf, unit_vec, inverse, gain_rows):
    grad_normed = grad_normed_bf.astype(jnp.float32)
    gain_part = jnp.sum(grad_normed * unit_vec, axis=(1, 2, 3))
    grad_unit = grad_normed * gain_rows
    grad_raw = inverse * (
        grad_unit - unit_vec * jnp.mean(grad_unit * unit_vec, axis=-1, keepdims=True)
    )
    return (grad_raw.astype(jnp.bfloat16), gain_part)


def global_position(local_row, owner_index, text_rows, text_group, image_rows, grp_count):
    text_place = (
        local_row // text_group * grp_count + owner_index
    ) * text_group + local_row % text_group
    image_place = TXT + owner_index * image_rows + (local_row - text_rows)
    return jnp.where(local_row < text_rows, text_place, image_place)


def per_device(text_proj, image_proj, text_grad, image_grad, text_lengths, norm_gains):
    seq_count = lax.axis_size("seq")
    grp_count = lax.axis_size("grp")
    sample_count, head_count, image_rows, head_size = image_grad.shape
    text_group = text_proj.shape[3]
    text_rows = text_group * seq_count
    local_len = text_rows + image_rows
    text_unit, text_inverse = unit_parts(text_proj[:2])
    image_unit, image_inverse = unit_parts(image_proj[:2])
    text_gain = norm_gains[0][:, None, None, None, :]
    image_gain = norm_gains[1][:, None, None, None, :]
    text_stack = jnp.concatenate(
        [(text_unit * text_gain).astype(jnp.bfloat16), text_proj[2:]], axis=0
    )
    image_stack = jnp.concatenate(
        [(image_unit * image_gain).astype(jnp.bfloat16), image_proj[2:]], axis=0
    )
    text_here, text_cot = (
        lax.all_to_all(text_stack, "seq", split_axis=1, concat_axis=3, tiled=True),
        lax.all_to_all(text_grad[None], "seq", split_axis=1, concat_axis=3, tiled=True),
    )
    joint_rows = jnp.concatenate([text_here, image_stack], axis=3)
    cotangent_rows = jnp.concatenate([text_cot[0], image_grad], axis=2)
    key_row = jnp.arange(local_len * grp_count, dtype=jnp.int32)
    key_place = global_position(
        key_row % local_len, key_row // local_len, text_rows, text_group, image_rows, grp_count
    )
    key_valid = (key_place[None, :] >= TXT) | (key_place[None, :] < text_lengths[:, None])
    full_len = local_len * grp_count
    moved_rows, moved_cot = (
        lax.all_to_all(joint_rows, "grp", split_axis=2, concat_axis=3, tiled=True),
        lax.all_to_all(cotangent_rows[None], "grp", split_axis=2, concat_axis=3, tiled=True),
    )
    head_share = moved_rows.shape[2]
    item_count = sample_count * head_share
    flat_rows = moved_rows.reshape(3, item_count, full_len, head_size)
    item_valid = jnp.broadcast_to(
        key_valid[:, None, :], (sample_count, head_share, full_len)
    ).reshape(item_count, full_len)
    attn_local, grad_query, grad_key, grad_value = lax.map(
        whole_item,
        (
            flat_rows[0],
            flat_rows[1],
            flat_rows[2],
            item_valid,
            moved_cot.reshape(item_count, full_len, head_size),
        ),
    )
    results = jnp.stack([attn_local, grad_query, grad_key, grad_value]).reshape(
        4, sample_count, head_share, full_len, head_size
    )
    placed = lax.all_to_all(results, "grp", split_axis=3, concat_axis=2, tiled=True)
    text_back = lax.all_to_all(
        placed[:, :, :, :text_rows], "seq", split_axis=3, concat_axis=1, tiled=True
    )
    image_back = placed[:, :, :, text_rows:]
    text_raw, text_part = raw_gradient(text_back[1:3], text_unit, text_inverse, text_gain)
    image_raw, image_part = raw_gradient(image_back[1:3], image_unit, image_inverse, image_gain)
    partial_value = jnp.stack([text_part, image_part])
    summed_gain = lax.psum(partial_value, ("dp", "seq", "grp"))
    gain_grad = summed_gain / (sample_count * lax.axis_size("dp") * seq_count)
    text_proj_grad = jnp.concatenate([text_raw, text_back[3:]], axis=0)
    image_proj_grad = jnp.concatenate([image_raw, image_back[3:]], axis=0)
    return (text_back[0], image_back[0], text_proj_grad, image_proj_grad, gain_grad)


def solution(mesh):
    placed = (
        P(None, "dp", None, ("seq", "grp"), None),
        P(None, ("dp", "seq"), None, "grp", None),
        P("dp", None, ("seq", "grp"), None),
        P(("dp", "seq"), None, "grp", None),
        P(("dp", "seq")),
        P(),
    )
    return jax.shard_map(
        per_device,
        mesh=mesh,
        in_specs=placed,
        out_specs=(
            P("dp", None, ("seq", "grp"), None),
            P(("dp", "seq"), None, "grp", None),
            P(None, "dp", None, ("seq", "grp"), None),
            P(None, ("dp", "seq"), None, "grp", None),
            P(),
        ),
        check_vma=False,
    )
```

profile of v0, /device:TPU:10, one launch (start us, length us, event | category | flops | bytes accessed | tf_op | source)
XLA Modules:
  0.0 161.8 jit_solution(1333477667918705269)
XLA Ops:
  0.6 5.5 %all-to-all-start.2 = ((bf16[1,4,12,16,128]{4,3,2,0,1:T(8,128)(2,1)}), bf16[1,4,12,16,128]{4,3,2,0,1:T(8,128)(2,1)S(1)}, u32[]{:S(2)}, u32[]{:S(2)}) async-start(bf16[1,4,12,16,128]{4,3,2,0,1:T(8,128)(2,1)} %bitcast.157), calls=%async_computation.2 | async-start | bytes 393216 | tf_op jit(solution)/shard_map/all_to_all | solution.py:103
  6.1 0.7 slice_bitcast_fusion.6
  6.8 1.3 fusion.56
  8.1 1.3 fusion.54
  10.2 1.0 copy.85
  11.2 0.9 all-to-all-done.2
  12.1 4.1 %all_to_all.96 = bf16[1,1,12,144,128]{4,3,1,0,2:T(8,128)(2,1)S(1)} all-to-all(bf16[1,1,12,144,128]{4,3,1,0,2:T(8,128)(2,1)S(1)} %maximum_bitcast_fusion.1), channel_id=1, replica_groups=mesh['dp'=4,'seq'=4,'grp'=2] {'grp'}, dimensions={2} | all-to-all | bytes 884736 | tf_op jit(solution)/shard_map/all_to_all | solution.py:115
  16.2 5.0 %all-to-all-start = ((bf16[3,4,12,16,128]{4,3,2,0,1:T(8,128)(2,1)}), bf16[3,4,12,16,128]{4,3,2,0,1:T(8,128)(2,1)S(1)}, u32[]{:S(2)}, u32[]{:S(2)}) async-start(bf16[3,4,12,16,128]{4,3,2,0,1:T(8,128)(2,1)} %copy.85), calls=%async_computation | async-start | bytes 1179648 | tf_op jit(solution)/shard_map/all_to_all | solution.py:102
  21.3 0.5 fusion.46
  21.8 0.3 fusion.44
  22.2 0.8 copy.94
  23.0 11.4 %all-to-all-done = bf16[3,4,12,16,128]{4,3,2,0,1:T(8,128)(2,1)S(1)} async-done(((bf16[3,4,12,16,128]{4,3,2,0,1:T(8,128)(2,1)}), bf16[3,4,12,16,128]{4,3,2,0,1:T(8,128)(2,1)S(1)}, u32[]{:S(2)}, u32[]{:S(2)}) %all-to-all-start) | async-done | bytes 589856 | tf_op jit(solution)/shard_map/all_to_all | solution.py:102
  34.7 4.8 %all_to_all.97 = bf16[3,1,12,144,128]{4,3,1,0,2:T(8,128)(2,1)S(1)} all-to-all(bf16[3,1,12,144,128]{4,3,1,0,2:T(8,128)(2,1)S(1)} %maximum_maximum_fusion), channel_id=1, replica_groups=mesh['dp'=4,'seq'=4,'grp'=2] {'grp'}, dimensions={2} | all-to-all | bytes 2654208 | tf_op jit(solution)/shard_map/all_to_all | solution.py:114
  39.7 0.9 copy-done.2
  40.6 32.7 %while.16 = (s32[]{:T(128)}, bf16[6,288,128]{2,1,0:T(8,128)(2,1)}, bf16[6,288,128]{2,1,0:T(8,128)(2,1)}, bf16[6,288,128]{2,1,0:T(8,128)(2,1)}, bf16[6,288,128]{2...) while((s32[]{:T(128)}, bf16[6,288,128]{2,1,0:T(8,128)(2,1)}, ...), condition=%wide.region_6.7_spmd, body=%wide.region_2.6_spmd.sunk | while | flops 129290400 | bytes 4506681 | solution.py:123
  40.6 0.2 fusion.111
  40.9 1.1 fusion.116
  42.1 0.9 fusion.113
  43.0 1.1 multiply_reduce_fusion.2
  44.3 0.9 fusion.115
  45.1 0.9 fusion.114
  46.4 1.1 fusion.116
  47.5 0.9 fusion.113
  48.4 1.1 multiply_reduce_fusion.2
  49.7 0.9 fusion.115
  50.6 0.9 fusion.114
  51.8 1.1 fusion.116
  53.0 0.9 fusion.113
  53.9 1.1 multiply_reduce_fusion.2
  55.2 0.9 fusion.115
  56.0 0.9 fusion.114
  57.3 1.1 fusion.116
  58.4 0.9 fusion.113
  59.3 1.1 multiply_reduce_fusion.2
  60.6 0.8 fusion.115
  61.5 0.9 fusion.114
  62.7 1.1 fusion.116
  63.9 0.9 fusion.113
  64.8 1.1 multiply_reduce_fusion.2
  66.0 0.9 fusion.115
  66.9 0.9 fusion.114
  68.2 1.1 fusion.116
  69.3 0.9 fusion.113
  70.2 1.1 multiply_reduce_fusion.2
  71.5 0.9 fusion.115
  72.4 0.9 fusion.114
  73.3 1.5 maximum_bitcast_fusion
  74.8 1.4 copy.95
  76.1 5.2 %all_to_all.98 = bf16[4,1,6,288,128]{4,0,2,1,3:T(4,128)(2,1)S(1)} all-to-all(bf16[4,1,6,288,128]{4,0,2,1,3:T(4,128)(2,1)S(1)} %copy.95), channel_id=1, replica_groups=mesh['dp'=4,'seq'=4,'grp'=2] {'grp'}, dimensions={3} | all-to-all | bytes 3538944 | tf_op jit(solution)/shard_map/all_to_all | solution.py:136
  81.3 0.3 copy.96
  81.7 1.6 copy.97
  83.3 7.5 %all-to-all-start.5 = ((bf16[4,1,12,64,128]{4,2,1,0,3:T(8,128)(2,1)}), bf16[4,1,12,64,128]{4,2,1,0,3:T(8,128)(2,1)}, u32[]{:S(2)}, u32[]{:S(2)}) async-start(bf16[4,1,12,64,128]{4,2,1,0,3:T(8,128)(2,1)} %copy.97), calls=%async_computation.5 | async-start | bytes 2097152 | tf_op jit(solution)/shard_map/all_to_all | solution.py:137
  90.7 0.9 fusion.47
  91.6 0.7 fusion.73
  92.3 0.7 fusion.43
  93.1 0.9 copy.101
  94.0 19.8 %all-to-all-done.5 = bf16[4,1,12,64,128]{4,2,1,0,3:T(8,128)(2,1)} async-done(((bf16[4,1,12,64,128]{4,2,1,0,3:T(8,128)(2,1)}), bf16[4,1,12,64,128]{4,2,1,0,3:T(8,128)(2,1)}, u32[]{:S(2)}, u32[]{:S(2)}) %all-to-all-start.5) | async-done | bytes 786464 | tf_op jit(solution)/shard_map/all_to_all | solution.py:137
  113.8 1.7 %copy.98 = bf16[4,1,12,64,128]{4,3,2,0,1:T(8,128)(2,1)S(1)} copy(bf16[4,1,12,64,128]{4,2,1,0,3:T(8,128)(2,1)} %all-to-all-done.5) | data formatting | bytes 1572864 | tf_op jit(solution)/shard_map/all_to_all | solution.py:137
  115.5 0.6 fusion.57
  116.1 42.8 %psum.7 = f32[2,2,128]{2,1,0:T(2,128)S(1)} all-reduce(f32[2,2,128]{2,1,0:T(2,128)S(1)} %pad_maximum_fusion.3), channel_id=1, replica_groups=mesh['dp'=4,'seq'=4,'grp'=2] {'dp','seq','grp'}, use_global_device_ids=true, to_apply=%region_11.12 | all-reduce | flops 512 | bytes 4096 | tf_op jit(solution)/shard_map/psum | solution.py:144
  159.0 0.6 broadcast_multiply_fusion.2
  159.6 0.5 fusion.53
  160.1 1.0 copy.100
  161.1 0.7 copy.99
  (55 shorter events, 3.7 us)
Async XLA Ops:
  0.6 9.5 %copy-start.1 = (bf16[3,4,12,16,128]{4,3,2,1,0:T(8,128)(2,1)S(1)}, bf16[3,4,12,16,128]{4,3,2,1,0:T(8,128)(2,1)}, u32[]{:S(2)}) copy-start(bf16[3,4,12,16,128]{4,3,2,1,0:T(8,128)(2,1)} %param.8) | copy-start | bytes 1769476
  0.6 11.4 %all-to-all-start.2 = ((bf16[1,4,12,16,128]{4,3,2,0,1:T(8,128)(2,1)}), bf16[1,4,12,16,128]{4,3,2,0,1:T(8,128)(2,1)S(1)}, u32[]{:S(2)}, u32[]{:S(2)}) async-start(bf16[1,4,12,16,128]{4,3,2,0,1:T(8,128)(2,1)} %bitcast.157), calls=%async_computation.2 | async-start | bytes 393216 | tf_op jit(solution)/shard_map/all_to_all | solution.py:103
  8.1 4.0 %copy-start.3 = (bf16[1,12,80,128]{3,2,1,0:T(8,128)(2,1)S(1)}, bf16[1,12,80,128]{3,2,1,0:T(8,128)(2,1)}, u32[]{:S(2)}) copy-start(bf16[1,12,80,128]{3,2,1,0:T(8,128)(2,1)} %param.11) | copy-start | bytes 737284
  11.2 10.1 %copy-start = (bf16[3,1,12,80,128]{4,3,2,1,0:T(8,128)(2,1)S(1)}, bf16[3,1,12,80,128]{4,3,2,1,0:T(8,128)(2,1)}, u32[]{:S(2)}) copy-start(bf16[3,1,12,80,128]{4,3,2,1,0:T(8,128)(2,1)} %param.9) | copy-start | bytes 2211844
  16.2 18.2 %all-to-all-start = ((bf16[3,4,12,16,128]{4,3,2,0,1:T(8,128)(2,1)}), bf16[3,4,12,16,128]{4,3,2,0,1:T(8,128)(2,1)S(1)}, u32[]{:S(2)}, u32[]{:S(2)}) async-start(bf16[3,4,12,16,128]{4,3,2,0,1:T(8,128)(2,1)} %copy.85), calls=%async_computation | async-start | bytes 1179648 | tf_op jit(solution)/shard_map/all_to_all | solution.py:102
  39.5 1.0 copy-start.2
  83.3 30.5 %all-to-all-start.5 = ((bf16[4,1,12,64,128]{4,2,1,0,3:T(8,128)(2,1)}), bf16[4,1,12,64,128]{4,2,1,0,3:T(8,128)(2,1)}, u32[]{:S(2)}, u32[]{:S(2)}) async-start(bf16[4,1,12,64,128]{4,2,1,0,3:T(8,128)(2,1)} %copy.97), calls=%async_computation.5 | async-start | bytes 2097152 | tf_op jit(solution)/shard_map/all_to_all | solution.py:137
where the time goes:
time: 163 us; the launch traced here: 162 us
  blocking collectives  56.9 us (35%)
  waiting for transfers between devices  32.1 us (20%)
  matrix products  31 us (19%)
  starting transfers between devices  17.9 us (11%)
  local copies, waits for them, and re-layouts  12.2 us (7%)
  other arithmetic  9.94 us (6%)
    psum x1, blocking collectives, per_device(): summed_gain = lax.psum(partial_value, ('dp', 'seq', 'grp'))  42.8 us
    all_to_all x1, waiting for transfers between devices, per_device(): lax.all_to_all(placed[:, :, :, :text_rows], 'seq', split_axis=3, concat_a...  19.8 us
    all_to_all x1, waiting for transfers between devices, per_device(): lax.all_to_all(text_stack, 'seq', split_axis=1, concat_axis=3, tiled=True)  11.4 us
    all_to_all x1, starting transfers between devices, per_device(): lax.all_to_all(placed[:, :, :, :text_rows], 'seq', split_axis=3, concat_a...  7.47 us
    dot_general x6, matrix products, backward_terms(): jnp.einsum('nqk,nqd->nkd', rounded_probs, grad_out, preferred_element_typ...  6.74 us
    dot_general x6, matrix products, backward_terms(): jnp.einsum('nqd,nkd->nqk', grad_out, value_rows, preferred_element_type=j...  6.74 us
    dot_general x6, matrix products, forward(): jnp.einsum('nqk,nkd->nqd', rounded_probs, value_rows, preferred_element_t...  5.55 us
    all_to_all x1, starting transfers between devices, per_device(): lax.all_to_all(text_grad[None], 'seq', split_axis=1, concat_axis=3, tiled...  5.46 us
  transfers between devices with their start and end apart: 3, of which 3 were waited for; matrix products, arithmetic and copies ran while one was open for 6% of the time, Pallas kernels for 0%

commit v1 on v0

--- a/solution.py
+++ b/solution.py
@@ -134,9 +134,20 @@
         4, sample_count, head_share, full_len, head_size
     )
     placed = lax.all_to_all(results, "grp", split_axis=3, concat_axis=2, tiled=True)
-    text_back = lax.all_to_all(
-        placed[:, :, :, :text_rows], "seq", split_axis=3, concat_axis=1, tiled=True
-    )
+    array = placed[:, :, :, :text_rows]
+    ways, here = (lax.axis_size("seq"), lax.axis_index("seq"))
+    width = array.shape[3] // ways
+    shape = list(array.shape)
+    shape[3] = width
+    height = shape[1]
+    shape[1] = height * ways
+    full = jnp.zeros(shape, array.dtype)
+    for mask in range(ways):
+        part = lax.dynamic_slice_in_dim(array, (here ^ mask) * width, width, axis=3)
+        if mask:
+            part = lax.ppermute(part, "seq", [(d, d ^ mask) for d in range(ways)])
+        full = lax.dynamic_update_slice_in_dim(full, part, (here ^ mask) * height, axis=1)
+    text_back = full
     image_back = placed[:, :, :, text_rows:]
     text_raw, text_part = raw_gradient(text_back[1:3], text_unit, text_inverse, text_gain)
     image_raw, image_part = raw_gradient(image_back[1:3], image_unit, image_inverse, image_gain)

time: 163 us -> 154 us (0.945)
  the two profiles are of different devices: /device:TPU:10 before, /device:TPU:0 now
where the time goes in v1:
time: 154 us; the launch traced here: 152 us
  blocking collectives  56.5 us (37%)
  matrix products  32.8 us (21%)
  waiting for transfers between devices  27.7 us (18%)
  starting transfers between devices  14.4 us (9%)
  other arithmetic  11.2 us (7%)
  local copies, waits for them, and re-layouts  7.86 us (5%)
  between operations  1.66 us (1%)
    psum x1, blocking collectives, per_device(): summed_gain = lax.psum(partial_value, ('dp', 'seq', 'grp'))  42.5 us
    all_to_all x1, waiting for transfers between devices, per_device(): lax.all_to_all(text_stack, 'seq', split_axis=1, concat_axis=3, tiled=True)  14 us
    dot_general x6, matrix products, backward_terms(): jnp.einsum('nqk,nqd->nkd', rounded_probs, grad_out, preferred_element_typ...  10.5 us
    ppermute x3, waiting for transfers between devices, per_device(): part = lax.ppermute(part, 'seq', [(d, d ^ mask) for d in range(ways)])  10.5 us
    dot_general x6, matrix products, forward(): jnp.einsum('nqk,nkd->nqd', rounded_probs, value_rows, preferred_element_t...  7.07 us
    dot_general x6, matrix products, backward_terms(): jnp.einsum('nqd,nkd->nqk', grad_out, value_rows, preferred_element_type=j...  6.98 us
    all_to_all x1, starting transfers between devices, per_device(): lax.all_to_all(text_grad[None], 'seq', split_axis=1, concat_axis=3, tiled...  6.49 us
    all_to_all x1, blocking collectives, per_device(): lax.all_to_all(results, 'grp', split_axis=3, concat_axis=2, tiled=True)  5.16 us
  transfers between devices with their start and end apart: 5, of which 4 were waited for; matrix products, arithmetic and copies ran while one was open for 5% of the time, Pallas kernels for 0%

profile of v1, /device:TPU:0, one launch (start us, length us, event | category | flops | bytes accessed | tf_op | source)
XLA Modules:
  0.0 152.5 jit_solution(6028886223841880279)
XLA Ops:
  0.6 6.5 %all-to-all-start.2 = ((bf16[1,4,12,16,128]{4,3,2,0,1:T(8,128)(2,1)}), bf16[1,4,12,16,128]{4,3,2,0,1:T(8,128)(2,1)S(1)}, u32[]{:S(2)}, u32[]{:S(2)}) async-start(bf16[1,4,12,16,128]{4,3,2,0,1:T(8,128)(2,1)} %bitcast.147), calls=%async_computation.2 | async-start | bytes 393216 | tf_op jit(solution)/shard_map/all_to_all | solution.py:103
  7.1 0.7 slice_bitcast_fusion.4
  7.9 1.3 fusion.56
  9.2 1.3 fusion.54
  10.5 0.9 pad_maximum_fusion
  11.4 3.3 %all-to-all-done.2 = bf16[1,4,12,16,128]{4,3,2,0,1:T(8,128)(2,1)S(1)} async-done(((bf16[1,4,12,16,128]{4,3,2,0,1:T(8,128)(2,1)}), bf16[1,4,12,16,128]{4,3,2,0,1:T(8,128)(2,1)S(1)}, u32[]{:S(2)}, u32[]{:S(2)}) %all-to-all-start.2) | async-done | bytes 196640 | tf_op jit(solution)/shard_map/all_to_all | solution.py:103
  14.7 4.1 %all_to_all.81 = bf16[1,1,12,144,128]{4,3,1,0,2:T(8,128)(2,1)S(1)} all-to-all(bf16[1,1,12,144,128]{4,3,1,0,2:T(8,128)(2,1)S(1)} %maximum_bitcast_fusion.2), channel_id=1, replica_groups=mesh['dp'=4,'seq'=4,'grp'=2] {'grp'}, dimensions={2} | all-to-all | bytes 884736 | tf_op jit(solution)/shard_map/all_to_all | solution.py:115
  18.8 3.5 %all-to-all-start = ((bf16[3,4,12,16,128]{4,3,2,0,1:T(8,128)(2,1)}), bf16[3,4,12,16,128]{4,3,2,0,1:T(8,128)(2,1)S(1)}, u32[]{:S(2)}, u32[]{:S(2)}) async-start(bf16[3,4,12,16,128]{4,3,2,0,1:T(8,128)(2,1)} %pad_maximum_fusion), calls=%async_computation | async-start | bytes 1179648 | tf_op jit(solution)/shard_map/all_to_all | solution.py:102
  23.1 0.5 fusion.46
  23.6 0.3 fusion.44
  23.9 0.8 copy.81
  24.7 14.0 %all-to-all-done = bf16[3,4,12,16,128]{4,3,2,0,1:T(8,128)(2,1)S(1)} async-done(((bf16[3,4,12,16,128]{4,3,2,0,1:T(8,128)(2,1)}), bf16[3,4,12,16,128]{4,3,2,0,1:T(8,128)(2,1)S(1)}, u32[]{:S(2)}, u32[]{:S(2)}) %all-to-all-start) | async-done | bytes 589856 | tf_op jit(solution)/shard_map/all_to_all | solution.py:102
  39.1 4.8 %all_to_all.82 = bf16[3,1,12,144,128]{4,3,1,0,2:T(8,128)(2,1)S(1)} all-to-all(bf16[3,1,12,144,128]{4,3,1,0,2:T(8,128)(2,1)S(1)} %copy.76), channel_id=1, replica_groups=mesh['dp'=4,'seq'=4,'grp'=2] {'grp'}, dimensions={2} | all-to-all | bytes 2654208 | tf_op jit(solution)/shard_map/all_to_all | solution.py:114
  44.0 0.8 copy.79
  45.0 0.3 copy-done.3
  45.2 34.6 %while.16 = (s32[]{:T(128)}, bf16[6,288,128]{2,1,0:T(8,128)(2,1)S(1)}, bf16[6,288,128]{2,1,0:T(8,128)(2,1)S(1)}, bf16[6,288,128]{2,1,0:T(8,128)(2,1)}, bf16[6,28...) while((s32[]{:T(128)}, ...), condition=%wide.region_6.7_spmd, body=%wide.region_2.6_spmd.sunk | while | flops 129290400 | bytes 4281905 | solution.py:123
  45.6 1.2 multiply_reduce_fusion.2
  46.9 0.9 fusion.108
  47.8 0.3 fusion.107
  48.1 1.7 %fusion.109 = bf16[6,288,128]{2,1,0:T(8,128)(2,1)} fusion(bf16[6,288,128]{2,1,0:T(8,128)(2,1)} %get-tuple-element.209, s32[]{:T(128)} %get-tuple-element.205, bf16[6,288,128]{2,1,0:T(8,128)(2,1)} %get-tuple-element.225, f32[288,288]{0,1:T(8,128)S(1)} %get-tuple-element.190, f32[288]{0:T(512)S(1)} %fusion.105, f32[288]{0:T(512)S(1)} %get-tuple-element.191), kind=kOutput, calls=%fused_computation.13.clone.1 | convolution fusion | flops 21519360 | bytes 482560 | tf_op jit(solution)/shard_map/while/body/eval_jaxpr/nqk,nqd->nkd/dot_general | solution.py:29
  49.8 1.2 fusion.106
  51.4 1.2 multiply_reduce_fusion.2
  52.7 0.9 fusion.108
  53.6 0.3 fusion.107
  53.8 1.8 %fusion.109 = bf16[6,288,128]{2,1,0:T(8,128)(2,1)} fusion(bf16[6,288,128]{2,1,0:T(8,128)(2,1)} %get-tuple-element.209, s32[]{:T(128)} %get-tuple-element.205, bf16[6,288,128]{2,1,0:T(8,128)(2,1)} %get-tuple-element.225, f32[288,288]{0,1:T(8,128)S(1)} %get-tuple-element.190, f32[288]{0:T(512)S(1)} %fusion.105, f32[288]{0:T(512)S(1)} %get-tuple-element.191), kind=kOutput, calls=%fused_computation.13.clone.1 | convolution fusion | flops 21519360 | bytes 482560 | tf_op jit(solution)/shard_map/while/body/eval_jaxpr/nqk,nqd->nkd/dot_general | solution.py:29
  55.6 1.2 fusion.106
  56.8 0.2 fusion.104
  57.2 1.2 multiply_reduce_fusion.2
  58.5 0.8 fusion.108
  59.3 0.3 fusion.107
  59.6 1.7 %fusion.109 = bf16[6,288,128]{2,1,0:T(8,128)(2,1)} fusion(bf16[6,288,128]{2,1,0:T(8,128)(2,1)} %get-tuple-element.209, s32[]{:T(128)} %get-tuple-element.205, bf16[6,288,128]{2,1,0:T(8,128)(2,1)} %get-tuple-element.225, f32[288,288]{0,1:T(8,128)S(1)} %get-tuple-element.190, f32[288]{0:T(512)S(1)} %fusion.105, f32[288]{0:T(512)S(1)} %get-tuple-element.191), kind=kOutput, calls=%fused_computation.13.clone.1 | convolution fusion | flops 21519360 | bytes 482560 | tf_op jit(solution)/shard_map/while/body/eval_jaxpr/nqk,nqd->nkd/dot_general | solution.py:29
  61.4 1.2 fusion.106
  62.9 1.2 multiply_reduce_fusion.2
  64.2 0.8 fusion.108
  65.1 0.3 fusion.107
  65.4 1.7 %fusion.109 = bf16[6,288,128]{2,1,0:T(8,128)(2,1)} fusion(bf16[6,288,128]{2,1,0:T(8,128)(2,1)} %get-tuple-element.209, s32[]{:T(128)} %get-tuple-element.205, bf16[6,288,128]{2,1,0:T(8,128)(2,1)} %get-tuple-element.225, f32[288,288]{0,1:T(8,128)S(1)} %get-tuple-element.190, f32[288]{0:T(512)S(1)} %fusion.105, f32[288]{0:T(512)S(1)} %get-tuple-element.191), kind=kOutput, calls=%fused_computation.13.clone.1 | convolution fusion | flops 21519360 | bytes 482560 | tf_op jit(solution)/shard_map/while/body/eval_jaxpr/nqk,nqd->nkd/dot_general | solution.py:29
  67.1 1.2 fusion.106
  68.7 1.2 multiply_reduce_fusion.2
  70.0 0.9 fusion.108
  70.9 0.3 fusion.107
  71.1 1.7 %fusion.109 = bf16[6,288,128]{2,1,0:T(8,128)(2,1)} fusion(bf16[6,288,128]{2,1,0:T(8,128)(2,1)} %get-tuple-element.209, s32[]{:T(128)} %get-tuple-element.205, bf16[6,288,128]{2,1,0:T(8,128)(2,1)} %get-tuple-element.225, f32[288,288]{0,1:T(8,128)S(1)} %get-tuple-element.190, f32[288]{0:T(512)S(1)} %fusion.105, f32[288]{0:T(512)S(1)} %get-tuple-element.191), kind=kOutput, calls=%fused_computation.13.clone.1 | convolution fusion | flops 21519360 | bytes 482560 | tf_op jit(solution)/shard_map/while/body/eval_jaxpr/nqk,nqd->nkd/dot_general | solution.py:29
  72.9 1.2 fusion.106
  74.5 1.2 multiply_reduce_fusion.2
  75.8 0.8 fusion.108
  76.6 0.3 fusion.107
  76.9 1.8 %fusion.109 = bf16[6,288,128]{2,1,0:T(8,128)(2,1)} fusion(bf16[6,288,128]{2,1,0:T(8,128)(2,1)} %get-tuple-element.209, s32[]{:T(128)} %get-tuple-element.205, bf16[6,288,128]{2,1,0:T(8,128)(2,1)} %get-tuple-element.225, f32[288,288]{0,1:T(8,128)S(1)} %get-tuple-element.190, f32[288]{0:T(512)S(1)} %fusion.105, f32[288]{0:T(512)S(1)} %get-tuple-element.191), kind=kOutput, calls=%fused_computation.13.clone.1 | convolution fusion | flops 21519360 | bytes 482560 | tf_op jit(solution)/shard_map/while/body/eval_jaxpr/nqk,nqd->nkd/dot_general | solution.py:29
  78.7 1.2 fusion.106
  79.9 1.4 maximum_bitcast_fusion
  81.2 1.4 copy.82
  82.6 5.2 %all_to_all.83 = bf16[4,1,6,288,128]{4,0,2,1,3:T(4,128)(2,1)S(1)} all-to-all(bf16[4,1,6,288,128]{4,0,2,1,3:T(4,128)(2,1)S(1)} %copy.82), channel_id=1, replica_groups=mesh['dp'=4,'seq'=4,'grp'=2] {'grp'}, dimensions={3} | all-to-all | bytes 3538944 | tf_op jit(solution)/shard_map/all_to_all | solution.py:136
  88.1 0.8 fusion.47
  89.4 2.0 %collective-permute-start.1 = (bf16[4,1,12,16,128]{4,3,2,0,1:T(8,128)(2,1)S(1)}, bf16[4,1,12,16,128]{4,3,2,0,1:T(8,128)(2,1)S(1)}, u32[]{:S(2)}, u32[]{:S(2)}) collective-permute-start(bf16[4,1,12,16,128]{4,3,2,0,1:T(8,128)(2,1)S(1)} %get-tuple-element.120), channel_id=1, source_target_pairs={{0,4},{2,6},{4,0},{6,2},{1,5},{3,7},{5,1},{7,3},{8,12},{10,14},{12... | collective-permute-start | bytes 589832 | tf_op jit(solution)/shard_map/ppermute | solution.py:148
  91.4 2.4 %collective-permute-start.2 = (bf16[4,1,12,16,128]{4,3,2,0,1:T(8,128)(2,1)S(1)}, bf16[4,1,12,16,128]{4,3,2,0,1:T(8,128)(2,1)S(1)}, u32[]{:S(2)}, u32[]{:S(2)}) collective-permute-start(bf16[4,1,12,16,128]{4,3,2,0,1:T(8,128)(2,1)S(1)} %get-tuple-element.119), channel_id=1, source_target_pairs={{0,6},{2,4},{4,2},{6,0},{1,7},{3,5},{5,3},{7,1},{8,14},{10,12},{12... | collective-permute-start | bytes 589832 | tf_op jit(solution)/shard_map/ppermute | solution.py:148
  93.7 0.7 fusion.43
  94.4 0.7 fusion.73
  95.1 0.9 maximum_bitcast_fusion.1
  96.1 3.2 %collective-permute-done = bf16[4,1,12,16,128]{4,3,2,0,1:T(8,128)(2,1)S(1)} collective-permute-done((bf16[4,1,12,16,128]{4,3,2,0,1:T(8,128)(2,1)S(1)}, bf16[4,1,12,16,128]{4,3,2,0,1:T(8,128)(2,1)S(1)}, u32[]{:S(2)}, u32[]{:S(2)}) %collective-permute-start) | collective-permute-done | bytes 196640 | tf_op jit(solution)/shard_map/ppermute | solution.py:148
  99.3 7.2 %collective-permute-done.1 = bf16[4,1,12,16,128]{4,3,2,0,1:T(8,128)(2,1)S(1)} collective-permute-done((bf16[4,1,12,16,128]{4,3,2,0,1:T(8,128)(2,1)S(1)}, bf16[4,1,12,16,128]{4,3,2,0,1:T(8,128)(2,1)S(1)}, u32[]{:S(2)}, u32[]{:S(2)}) %collective-permute-start.1) | collective-permute-done | bytes 196640 | tf_op jit(solution)/shard_map/ppermute | solution.py:148
  106.6 0.6 fusion.57
  107.2 0.7 fusion.75
  107.9 42.5 %psum.7 = f32[2,2,128]{2,1,0:T(2,128)S(1)} all-reduce(f32[2,2,128]{2,1,0:T(2,128)S(1)} %pad_maximum_fusion.2), channel_id=1, replica_groups=mesh['dp'=4,'seq'=4,'grp'=2] {'dp','seq','grp'}, use_global_device_ids=true, to_apply=%region_11.12 | all-reduce | flops 512 | bytes 4096 | tf_op jit(solution)/shard_map/psum | solution.py:155
  150.4 0.6 broadcast_multiply_fusion.2
  151.0 0.5 fusion.53
  151.6 0.9 copy.84
  (63 shorter events, 4.5 us)
Async XLA Ops:
  0.6 9.8 %copy-start.1 = (bf16[3,4,12,16,128]{4,3,2,1,0:T(8,128)(2,1)S(1)}, bf16[3,4,12,16,128]{4,3,2,1,0:T(8,128)(2,1)}, u32[]{:S(2)}) copy-start(bf16[3,4,12,16,128]{4,3,2,1,0:T(8,128)(2,1)} %param.8) | copy-start | bytes 1769476
  0.6 14.0 %all-to-all-start.2 = ((bf16[1,4,12,16,128]{4,3,2,0,1:T(8,128)(2,1)}), bf16[1,4,12,16,128]{4,3,2,0,1:T(8,128)(2,1)S(1)}, u32[]{:S(2)}, u32[]{:S(2)}) async-start(bf16[1,4,12,16,128]{4,3,2,0,1:T(8,128)(2,1)} %bitcast.147), calls=%async_computation.2 | async-start | bytes 393216 | tf_op jit(solution)/shard_map/all_to_all | solution.py:103
  7.1 7.5 %copy-start.4 = (bf16[1,12,80,128]{3,2,1,0:T(8,128)(2,1)S(1)}, bf16[1,12,80,128]{3,2,1,0:T(8,128)(2,1)}, u32[]{:S(2)}) copy-start(bf16[1,12,80,128]{3,2,1,0:T(8,128)(2,1)} %param.11) | copy-start | bytes 737284
  11.4 11.0 %copy-start = (bf16[3,1,12,80,128]{4,3,2,1,0:T(8,128)(2,1)S(1)}, bf16[3,1,12,80,128]{4,3,2,1,0:T(8,128)(2,1)}, u32[]{:S(2)}) copy-start(bf16[3,1,12,80,128]{4,3,2,1,0:T(8,128)(2,1)} %param.9) | copy-start | bytes 2211844
  18.8 19.9 %all-to-all-start = ((bf16[3,4,12,16,128]{4,3,2,0,1:T(8,128)(2,1)}), bf16[3,4,12,16,128]{4,3,2,0,1:T(8,128)(2,1)S(1)}, u32[]{:S(2)}, u32[]{:S(2)}) async-start(bf16[3,4,12,16,128]{4,3,2,0,1:T(8,128)(2,1)} %pad_maximum_fusion), calls=%async_computation | async-start | bytes 1179648 | tf_op jit(solution)/shard_map/all_to_all | solution.py:102
  43.9 1.0 copy-start.2
  43.9 1.3 copy-start.3
  89.3 10.0 %collective-permute-start = (bf16[4,1,12,16,128]{4,3,2,0,1:T(8,128)(2,1)S(1)}, bf16[4,1,12,16,128]{4,3,2,0,1:T(8,128)(2,1)S(1)}, u32[]{:S(2)}, u32[]{:S(2)}) collective-permute-start(bf16[4,1,12,16,128]{4,3,2,0,1:T(8,128)(2,1)S(1)} %get-tuple-element.121), channel_id=1, source_target_pairs={{0,2},{2,0},{4,6},{6,4},{1,3},{3,1},{5,7},{7,5},{8,10},{10,8},{12,... | collective-permute-start | bytes 589832 | tf_op jit(solution)/shard_map/ppermute | solution.py:148
  89.4 17.2 %collective-permute-start.1 = (bf16[4,1,12,16,128]{4,3,2,0,1:T(8,128)(2,1)S(1)}, bf16[4,1,12,16,128]{4,3,2,0,1:T(8,128)(2,1)S(1)}, u32[]{:S(2)}, u32[]{:S(2)}) collective-permute-start(bf16[4,1,12,16,128]{4,3,2,0,1:T(8,128)(2,1)S(1)} %get-tuple-element.120), channel_id=1, source_target_pairs={{0,4},{2,6},{4,0},{6,2},{1,5},{3,7},{5,1},{7,3},{8,12},{10,14},{12... | collective-permute-start | bytes 589832 | tf_op jit(solution)/shard_map/ppermute | solution.py:148
  91.4 15.2 %collective-permute-start.2 = (bf16[4,1,12,16,128]{4,3,2,0,1:T(8,128)(2,1)S(1)}, bf16[4,1,12,16,128]{4,3,2,0,1:T(8,128)(2,1)S(1)}, u32[]{:S(2)}, u32[]{:S(2)}) collective-permute-start(bf16[4,1,12,16,128]{4,3,2,0,1:T(8,128)(2,1)S(1)} %get-tuple-element.119), channel_id=1, source_target_pairs={{0,6},{2,4},{4,2},{6,0},{1,7},{3,5},{5,3},{7,1},{8,14},{10,12},{12... | collective-permute-start | bytes 589832 | tf_op jit(solution)/shard_map/ppermute | solution.py:148
